TPU v7x, 32 devices: a whole 2x2x4 slice. The times are simulated.
32 devices in a mesh: seq: 4 (over y, core), head: 8 (over z, x).
Axes of the slice: x: 2, y: 2, z: 4, core: 2. Of those that a mesh axis runs over, the one named last changes fastest.
Arguments:
- query: bfloat16 [4096, 4096], P(('seq', 'head')), may hold values from -6 to 6
- key_matrix: bfloat16 [4096, 2048], P(('seq', 'head')), may hold values from -6 to 6
- value_matrix: bfloat16 [4096, 2048], P(('seq', 'head')), may hold values from -6 to 6
- output_gradient: bfloat16 [4096, 4096], P(('seq', 'head')), may hold values from -6 to 6
- attn_out: bfloat16 [4096, 4096], P(('seq', 'head')), may hold values from -3 to 3
- doc_offsets: int32 [9], replicated, may hold values from 0 to 4096, as said below
- stats: float32 [4096, 32], P(('seq', 'head')), may hold values from -1 to 9
Outputs:
- grad_query: bfloat16 [4096, 4096], P(('seq', 'head'))
- key_gradient: bfloat16 [4096, 2048], P(('seq', 'head'))
- value_gradient: bfloat16 [4096, 2048], P(('seq', 'head'))
Inputs may be any that keep to these rules, and one draw needn't show every extreme that they name: doc_offsets[0] is 0, doc_offsets[8] is 4096, the entries rise strictly; no document has more than 1023 tokens and one has exactly that many.
All inputs are finite; a program needn't handle non-finite values.
Results may differ from a plain program's by a relative error of at most 0.0063.
Values may be sent and summed in bfloat16 or wider, within the bound.
A program may use at most 64 MiB of HBM per device.

v0:
```python
import jax
import jax.numpy as jnp
from jax import lax
from jax.sharding import PartitionSpec as P

HQ = 32
HEAD_SIZE = 128
DOCHALF = 512
QBLK = 512
attn_scale = 144.0 ** (-0.5)


def partner(value, axis, apart):
    mask = 2**apart
    pairs = [(source, source ^ mask) for source in range(lax.axis_size(axis))]
    return lax.ppermute(value, axis, pairs)


def from_behind(value, axis, steps):
    count = lax.axis_size(axis)
    leading, last = (max(0, -steps), min(count, count - steps))
    return lax.ppermute(value, axis, [(source, source + steps) for source in range(leading, last)])


def tile_grads(query_rows, grad_rows, lse_rows, delta_rows, key_window, value_window, allowed):
    score = (
        jnp.einsum("qgrd,kgd->grqk", query_rows, key_window, preferred_element_type=jnp.float32)
        * attn_scale
    )
    norm_stat = jnp.transpose(lse_rows, (1, 2, 0))[..., None]
    prob = jnp.where(allowed[None, None], jnp.exp(score - norm_stat), 0.0)
    dprob = jnp.einsum(
        "qgrd,kgd->grqk", grad_rows, value_window, preferred_element_type=jnp.float32
    )
    dscore = prob * (dprob - jnp.transpose(delta_rows, (1, 2, 0))[..., None])
    prob_low = prob.astype(jnp.bfloat16)
    dscore_low = dscore.astype(jnp.bfloat16)
    value_gradient = jnp.einsum(
        "grqk,qgrd->kgd", prob_low, grad_rows, preferred_element_type=jnp.float32
    )
    key_gradient = (
        jnp.einsum("grqk,qgrd->kgd", dscore_low, query_rows, preferred_element_type=jnp.float32)
        * attn_scale
    )
    grad_query = (
        jnp.einsum("grqk,kgd->qgrd", dscore_low, key_window, preferred_element_type=jnp.float32)
        * attn_scale
    )
    return (grad_query, key_gradient, value_gradient)


def doc_numbers(positions, inner):
    return jnp.sum((inner[None, :] <= positions[:, None]).astype(jnp.int32), axis=1)


def shards(query, key_matrix, value_matrix, output_gradient, attn_out, doc_offsets, stats):
    token_count_local = query.shape[0]
    members = lax.axis_size("head")
    group_span = token_count_local * members
    per_device = HQ // members
    lookback = 2 * DOCHALF
    width = lookback + QBLK
    group = lax.axis_index("seq")
    member = lax.axis_index("head")
    parity = member % 2
    half_width = HEAD_SIZE // 2
    delta_correction = jnp.sum(
        (output_gradient.astype(jnp.float32) * attn_out.astype(jnp.float32)).reshape(
            token_count_local, HQ, HEAD_SIZE
        ),
        axis=2,
    )
    query_heads, grad_heads = (
        lax.all_to_all(query, "head", split_axis=1, concat_axis=0, tiled=True),
        lax.all_to_all(output_gradient, "head", split_axis=1, concat_axis=0, tiled=True),
    )
    lse_heads, delta_heads = (
        lax.all_to_all(stats, "head", split_axis=1, concat_axis=0, tiled=True),
        lax.all_to_all(delta_correction, "head", split_axis=1, concat_axis=0, tiled=True),
    )
    key_cols, value_cols = (
        lax.all_to_all(key_matrix, "head", split_axis=1, concat_axis=0, tiled=True),
        lax.all_to_all(value_matrix, "head", split_axis=1, concat_axis=0, tiled=True),
    )
    if per_device >= 2:
        groups = per_device // 2
        key_heads = key_cols.reshape(group_span, groups, HEAD_SIZE)
        value_heads = value_cols.reshape(group_span, groups, HEAD_SIZE)
    else:
        groups = 1
        other_key, other_value = partner((key_cols, value_cols), "head", 0)
        key_heads = jnp.where(
            parity == 0,
            jnp.concatenate([key_cols, other_key], 1),
            jnp.concatenate([other_key, key_cols], 1),
        ).reshape(group_span, 1, HEAD_SIZE)
        value_heads = jnp.where(
            parity == 0,
            jnp.concatenate([value_cols, other_value], 1),
            jnp.concatenate([other_value, value_cols], 1),
        ).reshape(group_span, 1, HEAD_SIZE)
    repeats = per_device // groups
    query_heads = query_heads.reshape(group_span, groups, repeats, HEAD_SIZE)
    grad_heads = grad_heads.reshape(group_span, groups, repeats, HEAD_SIZE)
    lse_heads = lse_heads.reshape(group_span, groups, repeats)
    delta_heads = delta_heads.reshape(group_span, groups, repeats)
    prior_key, prior_value = from_behind(
        (key_heads[group_span - lookback :], value_heads[group_span - lookback :]), "seq", 1
    )
    key_ext = jnp.concatenate([prior_key, key_heads], 0)
    value_ext = jnp.concatenate([prior_value, value_heads], 0)
    inner = doc_offsets[1:-1]
    query_pos = group * group_span + jnp.arange(group_span, dtype=jnp.int32)
    key_pos = group * group_span - lookback + jnp.arange(lookback + group_span, dtype=jnp.int32)
    query_doc = doc_numbers(query_pos, inner)
    key_doc = doc_numbers(key_pos, inner)

    def block_step(block, carry):
        grad_q, grad_k, grad_v = carry
        start = (block * QBLK).astype(jnp.int32)
        query_rows = lax.dynamic_slice_in_dim(query_heads, start, QBLK, 0)
        grad_rows = lax.dynamic_slice_in_dim(grad_heads, start, QBLK, 0)
        lse_rows = lax.dynamic_slice_in_dim(lse_heads, start, QBLK, 0)
        delta_rows = lax.dynamic_slice_in_dim(delta_heads, start, QBLK, 0)
        key_window = lax.dynamic_slice_in_dim(key_ext, start, width, 0)
        value_window = lax.dynamic_slice_in_dim(value_ext, start, width, 0)
        rows_pos = lax.dynamic_slice_in_dim(query_pos, start, QBLK, 0)
        rows_doc = lax.dynamic_slice_in_dim(query_doc, start, QBLK, 0)
        cols_pos = lax.dynamic_slice_in_dim(key_pos, start, width, 0)
        cols_doc = lax.dynamic_slice_in_dim(key_doc, start, width, 0)
        allowed = (
            (cols_doc[None, :] == rows_doc[:, None])
            & (cols_pos[None, :] <= rows_pos[:, None])
            & (cols_pos[None, :] >= 0)
        )
        block_q, block_k, block_v = tile_grads(
            query_rows, grad_rows, lse_rows, delta_rows, key_window, value_window, allowed
        )
        grad_q = lax.dynamic_update_slice_in_dim(grad_q, block_q, start, 0)
        grad_k = lax.dynamic_update_slice_in_dim(
            grad_k, lax.dynamic_slice_in_dim(grad_k, start, width, 0) + block_k, start, 0
        )
        grad_v = lax.dynamic_update_slice_in_dim(
            grad_v, lax.dynamic_slice_in_dim(grad_v, start, width, 0) + block_v, start, 0
        )
        return (grad_q, grad_k, grad_v)

    init = (
        jnp.zeros((group_span, groups, repeats, HEAD_SIZE), jnp.float32),
        jnp.zeros((lookback + group_span, groups, HEAD_SIZE), jnp.float32),
        jnp.zeros((lookback + group_span, groups, HEAD_SIZE), jnp.float32),
    )
    grad_q, grad_k, grad_v = lax.fori_loop(0, group_span // QBLK, block_step, init)
    back_key, back_value = (
        from_behind(grad_k[:lookback].astype(jnp.bfloat16), "seq", -1).astype(jnp.float32),
        from_behind(grad_v[:lookback].astype(jnp.bfloat16), "seq", -1).astype(jnp.float32),
    )
    own_key = grad_k[lookback:].at[group_span - lookback :].add(back_key)
    own_value = grad_v[lookback:].at[group_span - lookback :].add(back_value)
    query_low = grad_q.astype(jnp.bfloat16).reshape(group_span, per_device * HEAD_SIZE)
    grad_query = lax.all_to_all(query_low, "head", split_axis=0, concat_axis=1, tiled=True)
    if per_device >= 2:
        send_key = own_key.reshape(group_span, groups * HEAD_SIZE)
        send_value = own_value.reshape(group_span, groups * HEAD_SIZE)
    else:
        flat_key = own_key.reshape(group_span, HEAD_SIZE)
        flat_value = own_value.reshape(group_span, HEAD_SIZE)
        keep_key = lax.dynamic_slice_in_dim(flat_key, parity * half_width, half_width, 1)
        keep_value = lax.dynamic_slice_in_dim(flat_value, parity * half_width, half_width, 1)
        give_key = lax.dynamic_slice_in_dim(flat_key, (1 - parity) * half_width, half_width, 1)
        give_value = lax.dynamic_slice_in_dim(flat_value, (1 - parity) * half_width, half_width, 1)
        from_key, from_value = partner((give_key, give_value), "head", 0)
        send_key = keep_key + from_key
        send_value = keep_value + from_value
    key_gradient_summed, value_gradient_summed = (
        lax.all_to_all(
            send_key.astype(jnp.bfloat16), "head", split_axis=0, concat_axis=1, tiled=True
        ).astype(send_key.dtype),
        lax.all_to_all(
            send_value.astype(jnp.bfloat16), "head", split_axis=0, concat_axis=1, tiled=True
        ).astype(send_value.dtype),
    )
    key_gradient = key_gradient_summed.astype(jnp.bfloat16)
    value_gradient = value_gradient_summed.astype(jnp.bfloat16)
    return (grad_query, key_gradient, value_gradient)


def solution(mesh):
    placed = (
        P(("seq", "head"), None),
        P(("seq", "head"), None),
        P(("seq", "head"), None),
        P(("seq", "head"), None),
        P(("seq", "head"), None),
        P(),
        P(("seq", "head"), None),
    )
    return jax.shard_map(
        shards,
        mesh=mesh,
        in_specs=placed,
        out_specs=(P(("seq", "head"), None), P(("seq", "head"), None), P(("seq", "head"), None)),
        check_vma=False,
    )
```

profile of v0, /device:TPU:1, one launch (start us, length us, event | category | flops | bytes accessed | tf_op | source)
XLA Modules:
  0.0 241.6 jit_solution(3520835461747851998)
XLA Ops:
  0.6 6.4 %all-to-all-start.2 = ((f32[128,8,4]{0,2,1:T(4,128)}), f32[128,8,4]{0,2,1:T(4,128)S(1)}, u32[]{:S(2)}, u32[]{:S(2)}) async-start(f32[128,8,4]{0,2,1:T(4,128)} %bitcast.171), calls=%async_computation.2 | async-start | bytes 32768 | tf_op jit(solution)/shard_map/all_to_all | solution.py:78
  12.4 3.5 %all-to-all-start.5 = ((f32[128,8,4]{0,2,1:T(4,128)}), f32[128,8,4]{0,2,1:T(4,128)S(1)}, u32[]{:S(2)}, u32[]{:S(2)}) async-start(f32[128,8,4]{0,2,1:T(4,128)} %bitcast.26), calls=%async_computation.5 | async-start | bytes 32768 | tf_op jit(solution)/shard_map/all_to_all | solution.py:79
  18.0 3.4 %all-to-all-done.5 = f32[128,8,4]{0,2,1:T(4,128)S(1)} async-done(((f32[128,8,4]{0,2,1:T(4,128)}), f32[128,8,4]{0,2,1:T(4,128)S(1)}, u32[]{:S(2)}, u32[]{:S(2)}) %all-to-all-start.5) | async-done | bytes 16416 | tf_op jit(solution)/shard_map/all_to_all | solution.py:79
  21.3 3.5 %all-to-all-start = ((bf16[128,8,256]{0,2,1:T(8,128)(2,1)}), bf16[128,8,256]{0,2,1:T(8,128)(2,1)S(1)}, u32[]{:S(2)}, u32[]{:S(2)}) async-start(bf16[128,8,256]{0,2,1:T(8,128)(2,1)} %bitcast.16), calls=%async_computation | async-start | bytes 1048576 | tf_op jit(solution)/shard_map/all_to_all | solution.py:82
  27.0 8.3 %all-to-all-done = bf16[128,8,256]{0,2,1:T(8,128)(2,1)S(1)} async-done(((bf16[128,8,256]{0,2,1:T(8,128)(2,1)}), bf16[128,8,256]{0,2,1:T(8,128)(2,1)S(1)}, u32[]{:S(2)}, u32[]{:S(2)}) %all-to-all-start) | async-done | bytes 524320 | tf_op jit(solution)/shard_map/all_to_all | solution.py:82
  35.3 6.5 %all-to-all-start.3 = ((bf16[128,8,256]{0,2,1:T(8,128)(2,1)}), bf16[128,8,256]{0,2,1:T(8,128)(2,1)S(1)}, u32[]{:S(2)}, u32[]{:S(2)}) async-start(bf16[128,8,256]{0,2,1:T(8,128)(2,1)} %bitcast.22), calls=%async_computation.3 | async-start | bytes 1048576 | tf_op jit(solution)/shard_map/all_to_all | solution.py:83
  43.2 11.9 %all-to-all-done.3 = bf16[128,8,256]{0,2,1:T(8,128)(2,1)S(1)} async-done(((bf16[128,8,256]{0,2,1:T(8,128)(2,1)}), bf16[128,8,256]{0,2,1:T(8,128)(2,1)S(1)}, u32[]{:S(2)}, u32[]{:S(2)}) %all-to-all-start.3) | async-done | bytes 524320 | tf_op jit(solution)/shard_map/all_to_all | solution.py:83
  55.9 4.2 %all-to-all-start.1 = ((bf16[128,8,512]{0,2,1:T(8,128)(2,1)}), bf16[128,8,512]{0,2,1:T(8,128)(2,1)S(1)}, u32[]{:S(2)}, u32[]{:S(2)}) async-start(bf16[128,8,512]{0,2,1:T(8,128)(2,1)} %bitcast.18), calls=%async_computation.1 | async-start | bytes 2097152 | tf_op jit(solution)/shard_map/all_to_all | solution.py:74
  61.4 23.0 %all-to-all-done.1 = bf16[128,8,512]{0,2,1:T(8,128)(2,1)S(1)} async-done(((bf16[128,8,512]{0,2,1:T(8,128)(2,1)}), bf16[128,8,512]{0,2,1:T(8,128)(2,1)S(1)}, u32[]{:S(2)}, u32[]{:S(2)}) %all-to-all-start.1) | async-done | bytes 1048608 | tf_op jit(solution)/shard_map/all_to_all | solution.py:74
  84.4 5.3 %all-to-all-start.4 = ((bf16[128,8,512]{0,2,1:T(8,128)(2,1)}), bf16[128,8,512]{0,2,1:T(8,128)(2,1)S(1)}, u32[]{:S(2)}, u32[]{:S(2)}) async-start(bf16[128,8,512]{0,2,1:T(8,128)(2,1)} %bitcast.24), calls=%async_computation.4 | async-start | bytes 2097152 | tf_op jit(solution)/shard_map/all_to_all | solution.py:75
  92.1 4.0 %collective-permute-start.1 = (bf16[1024,2,128]{0,2,1:T(8,128)(2,1)}, bf16[1024,2,128]{0,2,1:T(8,128)(2,1)}, u32[]{:S(2)}, u32[]{:S(2)}) collective-permute-start(bf16[1024,2,128]{0,2,1:T(8,128)(2,1)} %reshape.218), channel_id=1, source_target_pairs={{0,8},{8,16},{16,24},{1,9},{9,17},{17,25},{2,10},{10,18},{18,26},{... | collective-permute-start | bytes 1572872 | tf_op jit(solution)/shard_map/ppermute | solution.py:22
  119.6 48.6 %while.21 = (s32[]{:T(128)}, bf16[1024,2,2,128]{0,3,2,1:T(8,128)(2,1)}, f32[2048,2,128]{0,2,1:T(8,128)S(1)}, f32[2048,2,128]{0,2,1:T(8,128)}, bf16[2048,2,128]{0...) while((s32[]{:T(128)}, ...), condition=%wide.region_4.5_spmd, body=%wide.region_3.4_spmd.sunk | while | flops 4062578176 | bytes 158969360 | solution.py:153
  124.5 4.5 %copy-done = f32[2,1536,512,2]{2,1,3,0:T(8,128)} copy-done((f32[2,1536,512,2]{2,1,3,0:T(8,128)}, f32[2,1536,512,2]{2,1,3,0:T(8,128)S(1)}, u32[]{:S(2)}) %copy-start) | copy-done | bytes 12582936 | tf_op jit(solution)/shard_map/while
  132.3 8.1 %fusion.69 = bf16[2,2,512,1536]{2,3,1,0:T(8,128)(2,1)S(1)} fusion(f32[2,1536,512,2]{2,1,3,0:T(8,128)} %copy-done, f32[2,2,512]{2,1,0:T(2,128)S(1)} %get-tuple-element.474, f32[2,2,512]{2,1,0:T(2,128)S(1)} %get-tuple-element.475, pred[512,1536]{0,1:T(8,128)(4,1)S(1)} %and_and_fusion.2, bf16[2048,2,128]{0,2,1:T(8,128)(2,1)S(1)} %copy-done.13, ...), kind=kOutput, calls=%fused_computation.2.clone.1 | convolution fusion | flops 824180736 | bytes 20987912 | tf_op jit(solution)/shard_map/while/body/eval_jaxpr/qgrd,kgd->grqk/dot_general | solution.py:32
  148.9 4.5 %copy-done = f32[2,1536,512,2]{2,1,3,0:T(8,128)} copy-done((f32[2,1536,512,2]{2,1,3,0:T(8,128)}, f32[2,1536,512,2]{2,1,3,0:T(8,128)S(1)}, u32[]{:S(2)}) %copy-start) | copy-done | bytes 12582936 | tf_op jit(solution)/shard_map/while
  156.6 8.1 %fusion.69 = bf16[2,2,512,1536]{2,3,1,0:T(8,128)(2,1)S(1)} fusion(f32[2,1536,512,2]{2,1,3,0:T(8,128)} %copy-done, f32[2,2,512]{2,1,0:T(2,128)S(1)} %get-tuple-element.474, f32[2,2,512]{2,1,0:T(2,128)S(1)} %get-tuple-element.475, pred[512,1536]{0,1:T(8,128)(4,1)S(1)} %and_and_fusion.2, bf16[2048,2,128]{0,2,1:T(8,128)(2,1)S(1)} %copy-done.13, ...), kind=kOutput, calls=%fused_computation.2.clone.1 | convolution fusion | flops 824180736 | bytes 20987912 | tf_op jit(solution)/shard_map/while/body/eval_jaxpr/qgrd,kgd->grqk/dot_general | solution.py:32
  168.3 3.8 %collective-permute-start.2 = (bf16[1024,2,128]{0,2,1:T(8,128)(2,1)S(1)}, bf16[1024,2,128]{0,2,1:T(8,128)(2,1)S(1)}, u32[]{:S(2)}, u32[]{:S(2)}) collective-permute-start(bf16[1024,2,128]{0,2,1:T(8,128)(2,1)S(1)} %slice.67), channel_id=1, source_target_pairs={{8,0},{16,8},{24,16},{9,1},{17,9},{25,17},{10,2},{18,10},{26,18},{... | collective-permute-start | bytes 1572872 | tf_op jit(solution)/shard_map/ppermute | solution.py:22
  172.2 7.8 %collective-permute-done.2 = bf16[1024,2,128]{0,2,1:T(8,128)(2,1)S(1)} collective-permute-done((bf16[1024,2,128]{0,2,1:T(8,128)(2,1)S(1)}, bf16[1024,2,128]{0,2,1:T(8,128)(2,1)S(1)}, u32[]{:S(2)}, u32[]{:S(2)}) %collective-permute-start.2) | collective-permute-done | bytes 524320 | tf_op jit(solution)/shard_map/ppermute | solution.py:22
  181.3 3.9 %all-to-all-start.7 = ((bf16[8,128,256]{2,1,0:T(8,128)(2,1)}), bf16[8,128,256]{2,1,0:T(8,128)(2,1)S(1)}, u32[]{:S(2)}, u32[]{:S(2)}) async-start(bf16[8,128,256]{2,1,0:T(8,128)(2,1)} %copy.153), calls=%async_computation.7 | async-start | bytes 1048576 | tf_op jit(solution)/shard_map/all_to_all | solution.py:176
  188.6 8.6 %collective-permute-done.3 = bf16[1024,2,128]{0,2,1:T(8,128)(2,1)S(1)} collective-permute-done((bf16[1024,2,128]{0,2,1:T(8,128)(2,1)S(1)}, bf16[1024,2,128]{0,2,1:T(8,128)(2,1)S(1)}, u32[]{:S(2)}, u32[]{:S(2)}) %collective-permute-start.3) | collective-permute-done | bytes 524320 | tf_op jit(solution)/shard_map/ppermute | solution.py:22
  199.7 5.4 %all-to-all-start.8 = ((bf16[8,128,256]{2,1,0:T(8,128)(2,1)}), bf16[8,128,256]{2,1,0:T(8,128)(2,1)S(1)}, u32[]{:S(2)}, u32[]{:S(2)}) async-start(bf16[8,128,256]{2,1,0:T(8,128)(2,1)} %copy.154), calls=%async_computation.8 | async-start | bytes 1048576 | tf_op jit(solution)/shard_map/all_to_all | solution.py:179
  206.9 7.4 %all-to-all-done.8 = bf16[8,128,256]{2,1,0:T(8,128)(2,1)S(1)} async-done(((bf16[8,128,256]{2,1,0:T(8,128)(2,1)}), bf16[8,128,256]{2,1,0:T(8,128)(2,1)S(1)}, u32[]{:S(2)}, u32[]{:S(2)}) %all-to-all-start.8) | async-done | bytes 524320 | tf_op jit(solution)/shard_map/all_to_all | solution.py:179
  214.3 3.6 %all-to-all-start.6 = ((bf16[8,128,512]{2,1,0:T(8,128)(2,1)}), bf16[8,128,512]{2,1,0:T(8,128)(2,1)S(1)}, u32[]{:S(2)}, u32[]{:S(2)}) async-start(bf16[8,128,512]{2,1,0:T(8,128)(2,1)} %copy.152), calls=%async_computation.6 | async-start | bytes 2097152 | tf_op jit(solution)/shard_map/all_to_all | solution.py:161
  220.5 19.2 %all-to-all-done.6 = bf16[8,128,512]{2,1,0:T(8,128)(2,1)S(1)} async-done(((bf16[8,128,512]{2,1,0:T(8,128)(2,1)}), bf16[8,128,512]{2,1,0:T(8,128)(2,1)S(1)}, u32[]{:S(2)}, u32[]{:S(2)}) %all-to-all-start.6) | async-done | bytes 1048608 | tf_op jit(solution)/shard_map/all_to_all | solution.py:161
  (119 shorter events, 75.5 us)
Async XLA Ops:
  0.6 11.8 %all-to-all-start.2 = ((f32[128,8,4]{0,2,1:T(4,128)}), f32[128,8,4]{0,2,1:T(4,128)S(1)}, u32[]{:S(2)}, u32[]{:S(2)}) async-start(f32[128,8,4]{0,2,1:T(4,128)} %bitcast.171), calls=%async_computation.2 | async-start | bytes 32768 | tf_op jit(solution)/shard_map/all_to_all | solution.py:78
  9.2 32.7 %copy-start.12 = (bf16[128,4096]{1,0:T(8,128)(2,1)S(1)}, bf16[128,4096]{1,0:T(8,128)(2,1)}, u32[]{:S(2)}) copy-start(bf16[128,4096]{1,0:T(8,128)(2,1)} %param.17) | copy-start | bytes 3145732
  12.4 8.9 %all-to-all-start.5 = ((f32[128,8,4]{0,2,1:T(4,128)}), f32[128,8,4]{0,2,1:T(4,128)S(1)}, u32[]{:S(2)}, u32[]{:S(2)}) async-start(f32[128,8,4]{0,2,1:T(4,128)} %bitcast.26), calls=%async_computation.5 | async-start | bytes 32768 | tf_op jit(solution)/shard_map/all_to_all | solution.py:79
  21.3 14.0 %all-to-all-start = ((bf16[128,8,256]{0,2,1:T(8,128)(2,1)}), bf16[128,8,256]{0,2,1:T(8,128)(2,1)S(1)}, u32[]{:S(2)}, u32[]{:S(2)}) async-start(bf16[128,8,256]{0,2,1:T(8,128)(2,1)} %bitcast.16), calls=%async_computation | async-start | bytes 1048576 | tf_op jit(solution)/shard_map/all_to_all | solution.py:82
  24.8 35.2 %copy-start.7 = (bf16[128,4096]{1,0:T(8,128)(2,1)S(1)}, bf16[128,4096]{1,0:T(8,128)(2,1)}, u32[]{:S(2)}) copy-start(bf16[128,4096]{1,0:T(8,128)(2,1)} %param.20) | copy-start | bytes 3145732
  35.3 19.8 %copy-start.8 = (bf16[128,8,256]{0,2,1:T(8,128)(2,1)}, bf16[128,8,256]{0,2,1:T(8,128)(2,1)S(1)}, u32[]{:S(2)}) copy-start(bf16[128,8,256]{0,2,1:T(8,128)(2,1)S(1)} %all-to-all-done) | copy-start | bytes 1572868
  35.3 19.8 %all-to-all-start.3 = ((bf16[128,8,256]{0,2,1:T(8,128)(2,1)}), bf16[128,8,256]{0,2,1:T(8,128)(2,1)S(1)}, u32[]{:S(2)}, u32[]{:S(2)}) async-start(bf16[128,8,256]{0,2,1:T(8,128)(2,1)} %bitcast.22), calls=%async_computation.3 | async-start | bytes 1048576 | tf_op jit(solution)/shard_map/all_to_all | solution.py:83
  55.9 28.5 %all-to-all-start.1 = ((bf16[128,8,512]{0,2,1:T(8,128)(2,1)}), bf16[128,8,512]{0,2,1:T(8,128)(2,1)S(1)}, u32[]{:S(2)}, u32[]{:S(2)}) async-start(bf16[128,8,512]{0,2,1:T(8,128)(2,1)} %bitcast.18), calls=%async_computation.1 | async-start | bytes 2097152 | tf_op jit(solution)/shard_map/all_to_all | solution.py:74
  61.4 34.8 %copy-start.9 = (bf16[128,8,256]{0,2,1:T(8,128)(2,1)S(1)}, bf16[128,8,256]{0,2,1:T(8,128)(2,1)}, u32[]{:S(2)}) copy-start(bf16[128,8,256]{0,2,1:T(8,128)(2,1)} %copy-done.8) | copy-start | bytes 1572868
  84.4 14.5 %copy-start.15 = (s32[9]{0:T(128)S(1)}, s32[9]{0:T(128)}, u32[]{:S(2)}) copy-start(s32[9]{0:T(128)} %param.22) | copy-start | bytes 112
  84.4 30.4 %all-to-all-start.4 = ((bf16[128,8,512]{0,2,1:T(8,128)(2,1)}), bf16[128,8,512]{0,2,1:T(8,128)(2,1)S(1)}, u32[]{:S(2)}, u32[]{:S(2)}) async-start(bf16[128,8,512]{0,2,1:T(8,128)(2,1)} %bitcast.24), calls=%async_computation.4 | async-start | bytes 2097152 | tf_op jit(solution)/shard_map/all_to_all | solution.py:75
  92.1 10.4 %collective-permute-start.1 = (bf16[1024,2,128]{0,2,1:T(8,128)(2,1)}, bf16[1024,2,128]{0,2,1:T(8,128)(2,1)}, u32[]{:S(2)}, u32[]{:S(2)}) collective-permute-start(bf16[1024,2,128]{0,2,1:T(8,128)(2,1)} %reshape.218), channel_id=1, source_target_pairs={{0,8},{8,16},{16,24},{1,9},{9,17},{17,25},{2,10},{10,18},{18,26},{... | collective-permute-start | bytes 1572872 | tf_op jit(solution)/shard_map/ppermute | solution.py:22
  96.7 8.1 %copy-start.11 = (bf16[1024,2,128]{0,2,1:T(8,128)(2,1)}, bf16[1024,2,128]{0,2,1:T(8,128)(2,1)S(1)}, u32[]{:S(2)}) copy-start(bf16[1024,2,128]{0,2,1:T(8,128)(2,1)S(1)} %reshape.215) | copy-start | bytes 1572868
  96.8 11.3 %collective-permute-start = (bf16[1024,2,128]{0,2,1:T(8,128)(2,1)S(1)}, bf16[1024,2,128]{0,2,1:T(8,128)(2,1)}, u32[]{:S(2)}, u32[]{:S(2)}) collective-permute-start(bf16[1024,2,128]{0,2,1:T(8,128)(2,1)S(1)} %reshape.215), channel_id=1, source_target_pairs={{0,8},{8,16},{16,24},{1,9},{9,17},{17,25},{2,10},{10,18},{18,26},{... | collective-permute-start | bytes 1572872 | tf_op jit(solution)/shard_map/ppermute | solution.py:22
  132.2 8.1 %copy-start.3 = (f32[2048,2,128]{0,2,1:T(8,128)}, f32[2048,2,128]{0,2,1:T(8,128)S(1)}, u32[]{:S(2)}) copy-start(f32[2048,2,128]{0,2,1:T(8,128)S(1)} %fusion.72) | copy-start | bytes 6291460 | tf_op jit(solution)/shard_map/while
  132.3 8.1 %copy-start.4 = (bf16[1024,2,2,128]{0,3,2,1:T(8,128)(2,1)S(1)}, bf16[1024,2,2,128]{0,3,2,1:T(8,128)(2,1)}, u32[]{:S(2)}) copy-start(bf16[1024,2,2,128]{0,3,2,1:T(8,128)(2,1)} %get-tuple-element.498) | copy-start | bytes 3145732 | tf_op jit(solution)/shard_map/while
  156.6 8.1 %copy-start.3 = (f32[2048,2,128]{0,2,1:T(8,128)}, f32[2048,2,128]{0,2,1:T(8,128)S(1)}, u32[]{:S(2)}) copy-start(f32[2048,2,128]{0,2,1:T(8,128)S(1)} %fusion.72) | copy-start | bytes 6291460 | tf_op jit(solution)/shard_map/while
  156.6 8.1 %copy-start.4 = (bf16[1024,2,2,128]{0,3,2,1:T(8,128)(2,1)S(1)}, bf16[1024,2,2,128]{0,3,2,1:T(8,128)(2,1)}, u32[]{:S(2)}) copy-start(bf16[1024,2,2,128]{0,3,2,1:T(8,128)(2,1)} %get-tuple-element.498) | copy-start | bytes 3145732 | tf_op jit(solution)/shard_map/while
  168.3 11.6 %collective-permute-start.2 = (bf16[1024,2,128]{0,2,1:T(8,128)(2,1)S(1)}, bf16[1024,2,128]{0,2,1:T(8,128)(2,1)S(1)}, u32[]{:S(2)}, u32[]{:S(2)}) collective-permute-start(bf16[1024,2,128]{0,2,1:T(8,128)(2,1)S(1)} %slice.67), channel_id=1, source_target_pairs={{8,0},{16,8},{24,16},{9,1},{17,9},{25,17},{10,2},{18,10},{26,18},{... | collective-permute-start | bytes 1572872 | tf_op jit(solution)/shard_map/ppermute | solution.py:22
  181.3 18.4 %all-to-all-start.7 = ((bf16[8,128,256]{2,1,0:T(8,128)(2,1)}), bf16[8,128,256]{2,1,0:T(8,128)(2,1)S(1)}, u32[]{:S(2)}, u32[]{:S(2)}) async-start(bf16[8,128,256]{2,1,0:T(8,128)(2,1)} %copy.153), calls=%async_computation.7 | async-start | bytes 1048576 | tf_op jit(solution)/shard_map/all_to_all | solution.py:176
  185.2 19.9 %copy-start.6 = (bf16[1024,2,2,128]{0,3,2,1:T(8,128)(2,1)S(1)}, bf16[1024,2,2,128]{0,3,2,1:T(8,128)(2,1)}, u32[]{:S(2)}) copy-start(bf16[1024,2,2,128]{0,3,2,1:T(8,128)(2,1)} %get-tuple-element.274) | copy-start | bytes 3145732
  186.6 10.5 %collective-permute-start.3 = (bf16[1024,2,128]{0,2,1:T(8,128)(2,1)S(1)}, bf16[1024,2,128]{0,2,1:T(8,128)(2,1)S(1)}, u32[]{:S(2)}, u32[]{:S(2)}) collective-permute-start(bf16[1024,2,128]{0,2,1:T(8,128)(2,1)S(1)} %slice.66), channel_id=1, source_target_pairs={{8,0},{16,8},{24,16},{9,1},{17,9},{25,17},{10,2},{18,10},{26,18},{... | collective-permute-start | bytes 1572872 | tf_op jit(solution)/shard_map/ppermute | solution.py:22
  199.7 14.6 %all-to-all-start.8 = ((bf16[8,128,256]{2,1,0:T(8,128)(2,1)}), bf16[8,128,256]{2,1,0:T(8,128)(2,1)S(1)}, u32[]{:S(2)}, u32[]{:S(2)}) async-start(bf16[8,128,256]{2,1,0:T(8,128)(2,1)} %copy.154), calls=%async_computation.8 | async-start | bytes 1048576 | tf_op jit(solution)/shard_map/all_to_all | solution.py:179
  214.3 25.4 %all-to-all-start.6 = ((bf16[8,128,512]{2,1,0:T(8,128)(2,1)}), bf16[8,128,512]{2,1,0:T(8,128)(2,1)S(1)}, u32[]{:S(2)}, u32[]{:S(2)}) async-start(bf16[8,128,512]{2,1,0:T(8,128)(2,1)} %copy.152), calls=%async_computation.6 | async-start | bytes 2097152 | tf_op jit(solution)/shard_map/all_to_all | solution.py:161
  (13 other events, 53.6 us)
where the time goes:
time: 243 us; the launch traced here: 242 us
  waiting for transfers between devices  99.6 us (41%)
  starting transfers between devices  54.1 us (22%)
  local copies, waits for them, and re-layouts  40.6 us (17%)
  matrix products  35.3 us (15%)
  other arithmetic  10.8 us (4%)
    all_to_all x1, waiting for transfers between devices, shards(): lax.all_to_all(query, 'head', split_axis=1, concat_axis=0, tiled=True)  23 us
    ppermute x4, waiting for transfers between devices, from_behind(): lax.ppermute(value, axis, [(source, source + steps) for source in range(l...  22.9 us
    all_to_all x1, waiting for transfers between devices, shards(): lax.all_to_all(query_low, 'head', split_axis=0, concat_axis=1, tiled=True)  19.2 us
    dot_general x2, matrix products, tile_grads(): jnp.einsum('qgrd,kgd->grqk', grad_rows, value_window, preferred_element_t...  16.2 us
    all_to_all x1, waiting for transfers between devices, shards(): lax.all_to_all(value_matrix, 'head', split_axis=1, concat_axis=0, tiled=T...  11.9 us
    ppermute x4, starting transfers between devices, from_behind(): lax.ppermute(value, axis, [(source, source + steps) for source in range(l...  11.8 us
    unnamed x27, local copies, waits for them, and re-layouts  11.8 us
    while x32, local copies, waits for them, and re-layouts  9.4 us
  transfers between devices with their start and end apart: 13, of which 12 were waited for; matrix products, arithmetic and copies ran while one was open for 12% of the time, Pallas kernels for 0%

commit v1 on v0

--- a/solution.py
+++ b/solution.py
@@ -71,7 +71,12 @@
         axis=2,
     )
     query_heads, grad_heads = (
-        lax.all_to_all(query, "head", split_axis=1, concat_axis=0, tiled=True),
+        jnp.concatenate(
+            lax.all_to_all(
+                jnp.stack(jnp.split(query, lax.axis_size("head"), axis=1)), "head", 0, 0
+            ),
+            axis=0,
+        ),
         lax.all_to_all(output_gradient, "head", split_axis=1, concat_axis=0, tiled=True),
     )
     lse_heads, delta_heads = (

time: 243 us -> 242 us (level)
  local copies, waits for them, and re-layouts: 40.6 us -> 49.1 us
  waiting for transfers between devices: 99.6 us -> 91.8 us
    all_to_all x1, waiting for transfers between devices: 23 us -> 0.63 us  [shards(): lax.all_to_all(jnp.stack(jnp.split(query, lax.axis_size('head'), axis=1))...]
    all_to_all x1, waiting for transfers between devices: 1.49 us -> 16 us  [shards(): lax.all_to_all(output_gradient, 'head', split_axis=1, concat_axis=0, tile...]
    unnamed x27, local copies, waits for them, and re-layouts: 11.8 us -> 17 us
    dynamic_slice x0 -> x2, local copies, waits for them, and re-layouts: none -> 2.81 us  [block_step(): query_rows = lax.dynamic_slice_in_dim(query_heads, start, QBLK, 0)]
    while x32 -> x28, local copies, waits for them, and re-layouts: 9.4 us -> 9.08 us
  transfers between devices with their start and end apart: 13 -> 13, of which waited for: 12 -> 12; matrix products, arithmetic and copies ran while one was open for 12% -> 15% of each run, Pallas kernels for 0% -> 0%
where the time goes in v1:
time: 242 us; the launch traced here: 241 us
  waiting for transfers between devices  91.8 us (38%)
  starting transfers between devices  54.9 us (23%)
  local copies, waits for them, and re-layouts  49.1 us (20%)
  matrix products  33.1 us (14%)
  other arithmetic  10.9 us (5%)
    ppermute x4, waiting for transfers between devices, from_behind(): lax.ppermute(value, axis, [(source, source + steps) for source in range(l...  22.9 us
    all_to_all x1, waiting for transfers between devices, shards(): lax.all_to_all(query_low, 'head', split_axis=0, concat_axis=1, tiled=True)  19.2 us
    unnamed x27, local copies, waits for them, and re-layouts  17 us
    dot_general x2, matrix products, tile_grads(): jnp.einsum('qgrd,kgd->grqk', grad_rows, value_window, preferred_element_t...  16.2 us
    all_to_all x1, waiting for transfers between devices, shards(): lax.all_to_all(output_gradient, 'head', split_axis=1, concat_axis=0, tile...  16 us
    all_to_all x1, waiting for transfers between devices, shards(): lax.all_to_all(value_matrix, 'head', split_axis=1, concat_axis=0, tiled=T...  11.9 us
    ppermute x4, starting transfers between devices, from_behind(): lax.ppermute(value, axis, [(source, source + steps) for source in range(l...  11.9 us
    while x28, local copies, waits for them, and re-layouts  9.08 us
  transfers between devices with their start and end apart: 13, of which 12 were waited for; matrix products, arithmetic and copies ran while one was open for 15% of the time, Pallas kernels for 0%

profile of v1, /device:TPU:1, one launch (start us, length us, event | category | flops | bytes accessed | tf_op | source)
XLA Modules:
  0.0 241.0 jit_solution(16314894781380992240)
XLA Ops:
  0.6 6.4 %all-to-all-start.2 = ((f32[128,8,4]{0,2,1:T(4,128)}), f32[128,8,4]{0,2,1:T(4,128)S(1)}, u32[]{:S(2)}, u32[]{:S(2)}) async-start(f32[128,8,4]{0,2,1:T(4,128)} %bitcast.182), calls=%async_computation.2 | async-start | bytes 32768 | tf_op jit(solution)/shard_map/all_to_all | solution.py:83
  12.4 3.5 %all-to-all-start.5 = ((f32[128,8,4]{0,2,1:T(4,128)}), f32[128,8,4]{0,2,1:T(4,128)S(1)}, u32[]{:S(2)}, u32[]{:S(2)}) async-start(f32[128,8,4]{0,2,1:T(4,128)} %bitcast.32), calls=%async_computation.5 | async-start | bytes 32768 | tf_op jit(solution)/shard_map/all_to_all | solution.py:84
  18.0 3.4 %all-to-all-done.5 = f32[128,8,4]{0,2,1:T(4,128)S(1)} async-done(((f32[128,8,4]{0,2,1:T(4,128)}), f32[128,8,4]{0,2,1:T(4,128)S(1)}, u32[]{:S(2)}, u32[]{:S(2)}) %all-to-all-start.5) | async-done | bytes 16416 | tf_op jit(solution)/shard_map/all_to_all | solution.py:84
  21.3 3.5 %all-to-all-start = ((bf16[128,8,256]{0,2,1:T(8,128)(2,1)}), bf16[128,8,256]{0,2,1:T(8,128)(2,1)S(1)}, u32[]{:S(2)}, u32[]{:S(2)}) async-start(bf16[128,8,256]{0,2,1:T(8,128)(2,1)} %bitcast.16), calls=%async_computation | async-start | bytes 1048576 | tf_op jit(solution)/shard_map/all_to_all | solution.py:87
  26.9 8.4 %all-to-all-done = bf16[128,8,256]{0,2,1:T(8,128)(2,1)S(1)} async-done(((bf16[128,8,256]{0,2,1:T(8,128)(2,1)}), bf16[128,8,256]{0,2,1:T(8,128)(2,1)S(1)}, u32[]{:S(2)}, u32[]{:S(2)}) %all-to-all-start) | async-done | bytes 524320 | tf_op jit(solution)/shard_map/all_to_all | solution.py:87
  35.3 6.5 %all-to-all-start.3 = ((bf16[128,8,256]{0,2,1:T(8,128)(2,1)}), bf16[128,8,256]{0,2,1:T(8,128)(2,1)S(1)}, u32[]{:S(2)}, u32[]{:S(2)}) async-start(bf16[128,8,256]{0,2,1:T(8,128)(2,1)} %bitcast.28), calls=%async_computation.3 | async-start | bytes 1048576 | tf_op jit(solution)/shard_map/all_to_all | solution.py:88
  43.2 11.9 %all-to-all-done.3 = bf16[128,8,256]{0,2,1:T(8,128)(2,1)S(1)} async-done(((bf16[128,8,256]{0,2,1:T(8,128)(2,1)}), bf16[128,8,256]{0,2,1:T(8,128)(2,1)S(1)}, u32[]{:S(2)}, u32[]{:S(2)}) %all-to-all-start.3) | async-done | bytes 524320 | tf_op jit(solution)/shard_map/all_to_all | solution.py:88
  55.1 4.2 %all-to-all-start.4 = ((bf16[128,8,512]{0,2,1:T(8,128)(2,1)}), bf16[128,8,512]{0,2,1:T(8,128)(2,1)S(1)}, u32[]{:S(2)}, u32[]{:S(2)}) async-start(bf16[128,8,512]{0,2,1:T(8,128)(2,1)} %bitcast.30), calls=%async_computation.4 | async-start | bytes 2097152 | tf_op jit(solution)/shard_map/all_to_all | solution.py:80
  67.6 16.0 %all-to-all-done.4 = bf16[128,8,512]{0,2,1:T(8,128)(2,1)S(1)} async-done(((bf16[128,8,512]{0,2,1:T(8,128)(2,1)}), bf16[128,8,512]{0,2,1:T(8,128)(2,1)S(1)}, u32[]{:S(2)}, u32[]{:S(2)}) %all-to-all-start.4) | async-done | bytes 1048608 | tf_op jit(solution)/shard_map/all_to_all | solution.py:80
  83.6 5.2 %all-to-all-start.1 = ((bf16[8,128,512]{2,1,0:T(8,128)(2,1)}), bf16[8,128,512]{2,1,0:T(8,128)(2,1)S(1)}, u32[]{:S(2)}, u32[]{:S(2)}) async-start(bf16[8,128,512]{2,1,0:T(8,128)(2,1)} %copy-done.8), calls=%async_computation.1 | async-start | bytes 2097152 | tf_op jit(solution)/shard_map/all_to_all | solution.py:75
  92.0 4.0 %collective-permute-start.1 = (bf16[1024,2,128]{0,2,1:T(8,128)(2,1)}, bf16[1024,2,128]{0,2,1:T(8,128)(2,1)}, u32[]{:S(2)}, u32[]{:S(2)}) collective-permute-start(bf16[1024,2,128]{0,2,1:T(8,128)(2,1)} %reshape.210), channel_id=1, source_target_pairs={{0,8},{8,16},{16,24},{1,9},{9,17},{17,25},{2,10},{10,18},{18,26},{... | collective-permute-start | bytes 1572872 | tf_op jit(solution)/shard_map/ppermute | solution.py:22
  117.8 48.9 %while.21 = (s32[]{:T(128)}, bf16[1024,2,2,128]{0,3,2,1:T(8,128)(2,1)}, f32[2048,2,128]{0,2,1:T(8,128)S(1)}, f32[2048,2,128]{0,2,1:T(8,128)}, bf16[2048,2,128]{0...) while((s32[]{:T(128)}, ...), condition=%wide.region_4.5_spmd, body=%wide.region_3.4_spmd.sunk | while | flops 4062578176 | bytes 155823600 | solution.py:158
  123.0 4.5 %copy-done = f32[2,1536,512,2]{2,1,3,0:T(8,128)} copy-done((f32[2,1536,512,2]{2,1,3,0:T(8,128)}, f32[2,1536,512,2]{2,1,3,0:T(8,128)S(1)}, u32[]{:S(2)}) %copy-start) | copy-done | bytes 12582936 | tf_op jit(solution)/shard_map/while
  130.7 8.1 %fusion.68 = bf16[2,2,512,1536]{2,3,1,0:T(8,128)(2,1)S(1)} fusion(f32[2,1536,512,2]{2,1,3,0:T(8,128)} %copy-done, f32[2,2,512]{2,1,0:T(2,128)S(1)} %get-tuple-element.474, f32[2,2,512]{2,1,0:T(2,128)S(1)} %get-tuple-element.475, pred[512,1536]{0,1:T(8,128)(4,1)S(1)} %and_and_fusion.2, bf16[2048,2,128]{0,2,1:T(8,128)(2,1)S(1)} %copy-done.9, ...), kind=kOutput, calls=%fused_computation.2.clone.1 | convolution fusion | flops 824180736 | bytes 20987912 | tf_op jit(solution)/shard_map/while/body/eval_jaxpr/qgrd,kgd->grqk/dot_general | solution.py:32
  147.5 4.5 %copy-done = f32[2,1536,512,2]{2,1,3,0:T(8,128)} copy-done((f32[2,1536,512,2]{2,1,3,0:T(8,128)}, f32[2,1536,512,2]{2,1,3,0:T(8,128)S(1)}, u32[]{:S(2)}) %copy-start) | copy-done | bytes 12582936 | tf_op jit(solution)/shard_map/while
  155.2 8.1 %fusion.68 = bf16[2,2,512,1536]{2,3,1,0:T(8,128)(2,1)S(1)} fusion(f32[2,1536,512,2]{2,1,3,0:T(8,128)} %copy-done, f32[2,2,512]{2,1,0:T(2,128)S(1)} %get-tuple-element.474, f32[2,2,512]{2,1,0:T(2,128)S(1)} %get-tuple-element.475, pred[512,1536]{0,1:T(8,128)(4,1)S(1)} %and_and_fusion.2, bf16[2048,2,128]{0,2,1:T(8,128)(2,1)S(1)} %copy-done.9, ...), kind=kOutput, calls=%fused_computation.2.clone.1 | convolution fusion | flops 824180736 | bytes 20987912 | tf_op jit(solution)/shard_map/while/body/eval_jaxpr/qgrd,kgd->grqk/dot_general | solution.py:32
  166.9 3.8 %collective-permute-start.2 = (bf16[1024,2,128]{0,2,1:T(8,128)(2,1)S(1)}, bf16[1024,2,128]{0,2,1:T(8,128)(2,1)S(1)}, u32[]{:S(2)}, u32[]{:S(2)}) collective-permute-start(bf16[1024,2,128]{0,2,1:T(8,128)(2,1)S(1)} %slice.67), channel_id=1, source_target_pairs={{8,0},{16,8},{24,16},{9,1},{17,9},{25,17},{10,2},{18,10},{26,18},{... | collective-permute-start | bytes 1572872 | tf_op jit(solution)/shard_map/ppermute | solution.py:22
  170.7 7.7 %collective-permute-done.2 = bf16[1024,2,128]{0,2,1:T(8,128)(2,1)S(1)} collective-permute-done((bf16[1024,2,128]{0,2,1:T(8,128)(2,1)S(1)}, bf16[1024,2,128]{0,2,1:T(8,128)(2,1)S(1)}, u32[]{:S(2)}, u32[]{:S(2)}) %collective-permute-start.2) | collective-permute-done | bytes 524320 | tf_op jit(solution)/shard_map/ppermute | solution.py:22
  179.8 4.8 %all-to-all-start.7 = ((bf16[8,128,256]{2,1,0:T(8,128)(2,1)}), bf16[8,128,256]{2,1,0:T(8,128)(2,1)S(1)}, u32[]{:S(2)}, u32[]{:S(2)}) async-start(bf16[8,128,256]{2,1,0:T(8,128)(2,1)} %copy.152), calls=%async_computation.7 | async-start | bytes 1048576 | tf_op jit(solution)/shard_map/all_to_all | solution.py:181
  188.0 8.6 %collective-permute-done.3 = bf16[1024,2,128]{0,2,1:T(8,128)(2,1)S(1)} collective-permute-done((bf16[1024,2,128]{0,2,1:T(8,128)(2,1)S(1)}, bf16[1024,2,128]{0,2,1:T(8,128)(2,1)S(1)}, u32[]{:S(2)}, u32[]{:S(2)}) %collective-permute-start.3) | collective-permute-done | bytes 524320 | tf_op jit(solution)/shard_map/ppermute | solution.py:22
  199.1 5.4 %all-to-all-start.8 = ((bf16[8,128,256]{2,1,0:T(8,128)(2,1)}), bf16[8,128,256]{2,1,0:T(8,128)(2,1)S(1)}, u32[]{:S(2)}, u32[]{:S(2)}) async-start(bf16[8,128,256]{2,1,0:T(8,128)(2,1)} %copy.153), calls=%async_computation.8 | async-start | bytes 1048576 | tf_op jit(solution)/shard_map/all_to_all | solution.py:184
  206.3 7.4 %all-to-all-done.8 = bf16[8,128,256]{2,1,0:T(8,128)(2,1)S(1)} async-done(((bf16[8,128,256]{2,1,0:T(8,128)(2,1)}), bf16[8,128,256]{2,1,0:T(8,128)(2,1)S(1)}, u32[]{:S(2)}, u32[]{:S(2)}) %all-to-all-start.8) | async-done | bytes 524320 | tf_op jit(solution)/shard_map/all_to_all | solution.py:184
  213.7 3.6 %all-to-all-start.6 = ((bf16[8,128,512]{2,1,0:T(8,128)(2,1)}), bf16[8,128,512]{2,1,0:T(8,128)(2,1)S(1)}, u32[]{:S(2)}, u32[]{:S(2)}) async-start(bf16[8,128,512]{2,1,0:T(8,128)(2,1)} %copy.151), calls=%async_computation.6 | async-start | bytes 2097152 | tf_op jit(solution)/shard_map/all_to_all | solution.py:166
  219.9 19.2 %all-to-all-done.6 = bf16[8,128,512]{2,1,0:T(8,128)(2,1)S(1)} async-done(((bf16[8,128,512]{2,1,0:T(8,128)(2,1)}), bf16[8,128,512]{2,1,0:T(8,128)(2,1)S(1)}, u32[]{:S(2)}, u32[]{:S(2)}) %all-to-all-start.6) | async-done | bytes 1048608 | tf_op jit(solution)/shard_map/all_to_all | solution.py:166
  (117 shorter events, 81.1 us)
Async XLA Ops:
  0.6 11.8 %all-to-all-start.2 = ((f32[128,8,4]{0,2,1:T(4,128)}), f32[128,8,4]{0,2,1:T(4,128)S(1)}, u32[]{:S(2)}, u32[]{:S(2)}) async-start(f32[128,8,4]{0,2,1:T(4,128)} %bitcast.182), calls=%async_computation.2 | async-start | bytes 32768 | tf_op jit(solution)/shard_map/all_to_all | solution.py:83
  9.2 32.7 %copy-start.6 = (bf16[128,4096]{1,0:T(8,128)(2,1)S(1)}, bf16[128,4096]{1,0:T(8,128)(2,1)}, u32[]{:S(2)}) copy-start(bf16[128,4096]{1,0:T(8,128)(2,1)} %param.20) | copy-start | bytes 3145732
  12.4 8.9 %all-to-all-start.5 = ((f32[128,8,4]{0,2,1:T(4,128)}), f32[128,8,4]{0,2,1:T(4,128)S(1)}, u32[]{:S(2)}, u32[]{:S(2)}) async-start(f32[128,8,4]{0,2,1:T(4,128)} %bitcast.32), calls=%async_computation.5 | async-start | bytes 32768 | tf_op jit(solution)/shard_map/all_to_all | solution.py:84
  21.3 14.0 %all-to-all-start = ((bf16[128,8,256]{0,2,1:T(8,128)(2,1)}), bf16[128,8,256]{0,2,1:T(8,128)(2,1)S(1)}, u32[]{:S(2)}, u32[]{:S(2)}) async-start(bf16[128,8,256]{0,2,1:T(8,128)(2,1)} %bitcast.16), calls=%async_computation | async-start | bytes 1048576 | tf_op jit(solution)/shard_map/all_to_all | solution.py:87
  35.3 19.8 %all-to-all-start.3 = ((bf16[128,8,256]{0,2,1:T(8,128)(2,1)}), bf16[128,8,256]{0,2,1:T(8,128)(2,1)S(1)}, u32[]{:S(2)}, u32[]{:S(2)}) async-start(bf16[128,8,256]{0,2,1:T(8,128)(2,1)} %bitcast.28), calls=%async_computation.3 | async-start | bytes 1048576 | tf_op jit(solution)/shard_map/all_to_all | solution.py:88
  55.1 28.5 %all-to-all-start.4 = ((bf16[128,8,512]{0,2,1:T(8,128)(2,1)}), bf16[128,8,512]{0,2,1:T(8,128)(2,1)S(1)}, u32[]{:S(2)}, u32[]{:S(2)}) async-start(bf16[128,8,512]{0,2,1:T(8,128)(2,1)} %bitcast.30), calls=%async_computation.4 | async-start | bytes 2097152 | tf_op jit(solution)/shard_map/all_to_all | solution.py:80
  67.6 31.1 %copy-start.11 = (s32[9]{0:T(128)S(1)}, s32[9]{0:T(128)}, u32[]{:S(2)}) copy-start(s32[9]{0:T(128)} %param.22) | copy-start | bytes 112
  83.6 30.2 %all-to-all-start.1 = ((bf16[8,128,512]{2,1,0:T(8,128)(2,1)}), bf16[8,128,512]{2,1,0:T(8,128)(2,1)S(1)}, u32[]{:S(2)}, u32[]{:S(2)}) async-start(bf16[8,128,512]{2,1,0:T(8,128)(2,1)} %copy-done.8), calls=%async_computation.1 | async-start | bytes 2097152 | tf_op jit(solution)/shard_map/all_to_all | solution.py:75
  92.0 10.4 %collective-permute-start.1 = (bf16[1024,2,128]{0,2,1:T(8,128)(2,1)}, bf16[1024,2,128]{0,2,1:T(8,128)(2,1)}, u32[]{:S(2)}, u32[]{:S(2)}) collective-permute-start(bf16[1024,2,128]{0,2,1:T(8,128)(2,1)} %reshape.210), channel_id=1, source_target_pairs={{0,8},{8,16},{16,24},{1,9},{9,17},{17,25},{2,10},{10,18},{18,26},{... | collective-permute-start | bytes 1572872 | tf_op jit(solution)/shard_map/ppermute | solution.py:22
  96.6 8.1 %copy-start.7 = (bf16[1024,2,128]{0,2,1:T(8,128)(2,1)}, bf16[1024,2,128]{0,2,1:T(8,128)(2,1)S(1)}, u32[]{:S(2)}) copy-start(bf16[1024,2,128]{0,2,1:T(8,128)(2,1)S(1)} %reshape.208) | copy-start | bytes 1572868
  96.6 11.3 %collective-permute-start = (bf16[1024,2,128]{0,2,1:T(8,128)(2,1)S(1)}, bf16[1024,2,128]{0,2,1:T(8,128)(2,1)}, u32[]{:S(2)}, u32[]{:S(2)}) collective-permute-start(bf16[1024,2,128]{0,2,1:T(8,128)(2,1)S(1)} %reshape.208), channel_id=1, source_target_pairs={{0,8},{8,16},{16,24},{1,9},{9,17},{17,25},{2,10},{10,18},{18,26},{... | collective-permute-start | bytes 1572872 | tf_op jit(solution)/shard_map/ppermute | solution.py:22
  121.1 6.4 %copy-start.1 = (f32[2048,2,128]{0,2,1:T(8,128)S(1)}, f32[2048,2,128]{0,2,1:T(8,128)}, u32[]{:S(2)}) copy-start(f32[2048,2,128]{0,2,1:T(8,128)} %get-tuple-element.500) | copy-start | bytes 6291460 | tf_op jit(solution)/shard_map/while
  121.1 6.4 %copy-start.10 = (bf16[1024,2,2,128]{0,3,2,1:T(8,128)(2,1)S(1)}, bf16[1024,2,2,128]{0,3,2,1:T(8,128)(2,1)}, u32[]{:S(2)}) copy-start(bf16[1024,2,2,128]{0,3,2,1:T(8,128)(2,1)} %get-tuple-element.528) | copy-start | bytes 3145732 | tf_op jit(solution)/shard_map/while
  130.7 8.1 %copy-start.2 = (f32[2048,2,128]{0,2,1:T(8,128)}, f32[2048,2,128]{0,2,1:T(8,128)S(1)}, u32[]{:S(2)}) copy-start(f32[2048,2,128]{0,2,1:T(8,128)S(1)} %fusion.71) | copy-start | bytes 6291460 | tf_op jit(solution)/shard_map/while
  130.7 8.1 %copy-start.3 = (bf16[1024,2,2,128]{0,3,2,1:T(8,128)(2,1)S(1)}, bf16[1024,2,2,128]{0,3,2,1:T(8,128)(2,1)}, u32[]{:S(2)}) copy-start(bf16[1024,2,2,128]{0,3,2,1:T(8,128)(2,1)} %get-tuple-element.498) | copy-start | bytes 3145732 | tf_op jit(solution)/shard_map/while
  145.6 6.4 %copy-start.1 = (f32[2048,2,128]{0,2,1:T(8,128)S(1)}, f32[2048,2,128]{0,2,1:T(8,128)}, u32[]{:S(2)}) copy-start(f32[2048,2,128]{0,2,1:T(8,128)} %get-tuple-element.500) | copy-start | bytes 6291460 | tf_op jit(solution)/shard_map/while
  155.2 8.1 %copy-start.2 = (f32[2048,2,128]{0,2,1:T(8,128)}, f32[2048,2,128]{0,2,1:T(8,128)S(1)}, u32[]{:S(2)}) copy-start(f32[2048,2,128]{0,2,1:T(8,128)S(1)} %fusion.71) | copy-start | bytes 6291460 | tf_op jit(solution)/shard_map/while
  155.2 8.1 %copy-start.3 = (bf16[1024,2,2,128]{0,3,2,1:T(8,128)(2,1)S(1)}, bf16[1024,2,2,128]{0,3,2,1:T(8,128)(2,1)}, u32[]{:S(2)}) copy-start(bf16[1024,2,2,128]{0,3,2,1:T(8,128)(2,1)} %get-tuple-element.498) | copy-start | bytes 3145732 | tf_op jit(solution)/shard_map/while
  166.9 11.6 %collective-permute-start.2 = (bf16[1024,2,128]{0,2,1:T(8,128)(2,1)S(1)}, bf16[1024,2,128]{0,2,1:T(8,128)(2,1)S(1)}, u32[]{:S(2)}, u32[]{:S(2)}) collective-permute-start(bf16[1024,2,128]{0,2,1:T(8,128)(2,1)S(1)} %slice.67), channel_id=1, source_target_pairs={{8,0},{16,8},{24,16},{9,1},{17,9},{25,17},{10,2},{18,10},{26,18},{... | collective-permute-start | bytes 1572872 | tf_op jit(solution)/shard_map/ppermute | solution.py:22
  179.8 19.3 %all-to-all-start.7 = ((bf16[8,128,256]{2,1,0:T(8,128)(2,1)}), bf16[8,128,256]{2,1,0:T(8,128)(2,1)S(1)}, u32[]{:S(2)}, u32[]{:S(2)}) async-start(bf16[8,128,256]{2,1,0:T(8,128)(2,1)} %copy.152), calls=%async_computation.7 | async-start | bytes 1048576 | tf_op jit(solution)/shard_map/all_to_all | solution.py:181
  184.6 19.9 %copy-start.5 = (bf16[1024,2,2,128]{0,3,2,1:T(8,128)(2,1)S(1)}, bf16[1024,2,2,128]{0,3,2,1:T(8,128)(2,1)}, u32[]{:S(2)}) copy-start(bf16[1024,2,2,128]{0,3,2,1:T(8,128)(2,1)} %get-tuple-element.274) | copy-start | bytes 3145732
  186.0 10.5 %collective-permute-start.3 = (bf16[1024,2,128]{0,2,1:T(8,128)(2,1)S(1)}, bf16[1024,2,128]{0,2,1:T(8,128)(2,1)S(1)}, u32[]{:S(2)}, u32[]{:S(2)}) collective-permute-start(bf16[1024,2,128]{0,2,1:T(8,128)(2,1)S(1)} %slice.66), channel_id=1, source_target_pairs={{8,0},{16,8},{24,16},{9,1},{17,9},{25,17},{10,2},{18,10},{26,18},{... | collective-permute-start | bytes 1572872 | tf_op jit(solution)/shard_map/ppermute | solution.py:22
  199.1 14.6 %all-to-all-start.8 = ((bf16[8,128,256]{2,1,0:T(8,128)(2,1)}), bf16[8,128,256]{2,1,0:T(8,128)(2,1)S(1)}, u32[]{:S(2)}, u32[]{:S(2)}) async-start(bf16[8,128,256]{2,1,0:T(8,128)(2,1)} %copy.153), calls=%async_computation.8 | async-start | bytes 1048576 | tf_op jit(solution)/shard_map/all_to_all | solution.py:184
  213.7 25.4 %all-to-all-start.6 = ((bf16[8,128,512]{2,1,0:T(8,128)(2,1)}), bf16[8,128,512]{2,1,0:T(8,128)(2,1)S(1)}, u32[]{:S(2)}, u32[]{:S(2)}) async-start(bf16[8,128,512]{2,1,0:T(8,128)(2,1)} %copy.151), calls=%async_computation.6 | async-start | bytes 2097152 | tf_op jit(solution)/shard_map/all_to_all | solution.py:166
  (8 other events, 27.6 us)
